TPU v7x, 32 devices: a whole 2x2x4 slice. The times are simulated.
32 devices in a mesh: dp: 4 (over x, core), seq: 4 (over z), tensor: 2 (over y).
Axes of the slice: x: 2, y: 2, z: 4, core: 2. Of those that a mesh axis runs over, the one named last changes fastest.
Arguments:
- vit_out: bfloat16 [4096, 3200], P(('dp', 'seq')), may hold values from -6 to 6
- ln_gain: float32 [3200], replicated, may hold values from 0.1 to 1.9
- ln_bias: float32 [3200], replicated, may hold values from -3 to 3
- proj_weight: bfloat16 [3200, 4, 2048], P(None, None, 'tensor'), may hold values from -0.109375 to 0.109375
- proj_bias: float32 [4, 2048], P(None, 'tensor'), may hold values from -3 to 3
- text_embed: bfloat16 [16384, 8192], P('dp', ('seq', 'tensor')), may hold values from -6 to 6
- norm_gain: float32 [8192], P(('seq', 'tensor')), may hold values from 0.1 to 1.9
- tile_dest: int32 [32, 1], replicated, may hold values from 0 to 3; in each aligned block of 8 rows (0 to 7, 8 to 15, ...) at most 4 rows name the same one
- tile_place: int32 [4, 32], replicated, may hold values from 0 to 31, each once within a row
Outputs:
- normed: bfloat16 [16384, 8192], P('dp', ('seq', 'tensor'))
Inputs may be any that keep to these rules, and one draw needn't show every extreme that they name: `tile_dest`: in each aligned block of 8 rows (one encoder group's tiles) no replica is named more than 4 times, a bound that some block reaches. `tile_place`: each row is a permutation of 0 to 31.
All inputs are finite; a program needn't handle non-finite values.
Results may differ from a plain program's by a relative error of at most 0.0048.
Values may be sent and summed in bfloat16 or wider, within the bound.
A program may use at most 128 MiB of HBM per device.

v0:
```python
import jax
import jax.numpy as jnp
from jax import lax
from jax.sharding import PartitionSpec as P

D = 8192
TILE = 128


def layer_norm(rows, ln_gain, ln_bias):
    values = rows.astype(jnp.float32)
    center = values - jnp.mean(values, axis=-1, keepdims=True)
    spread = jnp.mean(center * center, axis=-1, keepdims=True)
    return (center * lax.rsqrt(spread + 1e-06) * ln_gain + ln_bias).astype(jnp.bfloat16)


def arrival_ranks(destination, replicas):
    onehot = (destination[:, None] == jnp.arange(replicas, dtype=jnp.int32)[None, :]).astype(
        jnp.int32
    )
    before = jnp.cumsum(onehot, axis=0) - onehot
    return jnp.sum(before * onehot, axis=1)


def row_squares(rows):
    values = rows.astype(jnp.float32)
    return jnp.sum(values * values, axis=-1)


def local(
    vit_out, ln_gain, ln_bias, proj_weight, proj_bias, text_embed, norm_gain, tile_dest, tile_place
):
    replicas = lax.axis_size("dp")
    owners = lax.axis_size("seq")
    my_replica = lax.axis_index("dp")
    local_rows = vit_out.shape[0]
    width_in = vit_out.shape[1]
    column_block = proj_weight.shape[2]
    positions = tile_place.shape[1]
    seq_rows = text_embed.shape[0]
    group_tiles = owners * local_rows // TILE
    total_tiles = tile_dest.shape[0]
    normed_in = layer_norm(vit_out, ln_gain, ln_bias)
    weights_flat = proj_weight.reshape(width_in, owners * column_block)
    hidden = jnp.dot(
        normed_in, weights_flat, preferred_element_type=jnp.float32
    ) + proj_bias.reshape(-1)
    projected = hidden.astype(jnp.bfloat16)
    regrouped = lax.all_to_all(
        projected.reshape(local_rows, owners, column_block),
        "seq",
        split_axis=1,
        concat_axis=0,
        tiled=True,
    )
    group_rows = regrouped.reshape(owners * local_rows, column_block)
    destination = tile_dest[:, 0]
    ranks = arrival_ranks(destination, replicas)
    place_row = lax.dynamic_index_in_dim(tile_place, my_replica, 0, keepdims=False)
    slot_of_tile = jnp.where(
        destination == my_replica, jnp.take(place_row, jnp.minimum(ranks, positions - 1)), -1
    )
    matches = slot_of_tile[None, :] == jnp.arange(positions, dtype=jnp.int32)[:, None]
    source_tile = (
        jnp.sum(
            matches.astype(jnp.int32) * (jnp.arange(total_tiles, dtype=jnp.int32) + 1)[None, :],
            axis=1,
        )
        - 1
    )
    text_tiles = text_embed.reshape(positions, TILE, column_block)
    capacity = max(2, 2 * group_tiles // replicas)
    local_dest = lax.dynamic_slice_in_dim(destination, my_replica * group_tiles, group_tiles)
    local_rank = arrival_ranks(local_dest, replicas)
    slot_index = local_dest * capacity + local_rank
    filling = slot_index[None, :] == jnp.arange(replicas * capacity, dtype=jnp.int32)[:, None]
    slot_source = (
        jnp.sum(
            filling.astype(jnp.int32) * (jnp.arange(group_tiles, dtype=jnp.int32) + 1)[None, :],
            axis=1,
        )
        - 1
    )
    tiles = group_rows.reshape(group_tiles, TILE, column_block)
    outgoing = jnp.where(
        (slot_source >= 0)[:, None, None],
        tiles[jnp.clip(slot_source, 0, group_tiles - 1)],
        jnp.zeros((), jnp.bfloat16),
    )
    outgoing = outgoing.reshape(replicas, capacity, TILE, column_block)
    incoming = lax.all_to_all(outgoing, "dp", split_axis=0, concat_axis=0, tiled=True).reshape(
        replicas * capacity, TILE, column_block
    )
    group_ranks = jax.vmap(lambda block: arrival_ranks(block, replicas))(
        destination.reshape(replicas, group_tiles)
    ).reshape(-1)
    safe_tile = jnp.clip(source_tile, 0, total_tiles - 1)
    arrival_index = safe_tile // group_tiles * capacity + jnp.take(group_ranks, safe_tile)
    picked = incoming[jnp.clip(arrival_index, 0, replicas * capacity - 1)]
    assembled = jnp.where((source_tile >= 0)[:, None, None], picked, text_tiles).reshape(
        seq_rows, column_block
    )
    squares = row_squares(assembled)
    totals = lax.psum(squares, ("seq", "tensor"))
    scale = lax.rsqrt(totals / D + 1e-05)
    return (assembled.astype(jnp.float32) * scale[:, None] * norm_gain).astype(jnp.bfloat16)


def solution(mesh):
    placed = (
        P(("dp", "seq"), None),
        P(),
        P(),
        P(None, None, "tensor"),
        P(None, "tensor"),
        P("dp", ("seq", "tensor")),
        P(("seq", "tensor")),
        P(),
        P(),
    )
    return jax.shard_map(
        local, mesh=mesh, in_specs=placed, out_specs=P("dp", ("seq", "tensor")), check_vma=False
    )
```

profile of v0, /device:TPU:0, one launch (start us, length us, event | category | flops | bytes accessed | tf_op | source)
XLA Modules:
  0.0 208.5 jit_solution(405158420390305600)
XLA Ops:
  0.0 0.0 copy-start
  0.0 0.0 copy-start.2
  0.0 0.0 copy-start.1
  0.0 0.0 copy-start.5
  0.0 0.0 copy-start.6
  0.0 18.2 %copy.13 = bf16[400,8,4,1024]{3,1,2,0:T(8,128)(2,1)} copy(bf16[400,8,4,1024]{3,2,1,0:T(4,128)(2,1)} %bitcast.39) | data formatting | bytes 52428800
  18.2 0.0 copy-done.2
  18.2 0.0 copy-done.1
  18.3 0.3 convert_reduce_fusion
  18.6 0.6 fusion.6
  19.2 0.0 copy-done.5
  19.2 0.0 copy-done.6
  19.2 12.3 %fusion.3 = bf16[256,4096]{1,0:T(8,128)(2,1)S(1)} fusion(bf16[3200,4096]{1,0:T(8,128)(2,1)} %bitcast.40, f32[4096]{0:T(1024)S(1)} %bitcast.46, bf16[256,3200]{1,0:T(8,128)(2,1)S(1)} %copy-done.1, f32[3200]{0:T(1024)S(1)} %copy-done.5, f32[3200]{0:T(1024)S(1)} %copy-done.6, f32[256]{0:T(256)S(1)} %add_rsqrt_fusion.1, f32[256]{0:T(256)S(1)} %broadcast_multiply_fusion), kind=kOutput, calls=%fused_computation.11 | convolution fusion | flops 6717898752 | bytes 29993984 | tf_op jit(solution)/shard_map/dot_general | solution.py:45
  31.5 0.0 copy-start.3
  31.5 1.5 copy.17
  33.0 6.4 %all-to-all-start = ((bf16[256,4,1024]{2,0,1:T(8,128)(2,1)}), bf16[256,4,1024]{2,0,1:T(8,128)(2,1)S(1)}, u32[]{:S(2)}, u32[]{:S(2)}) async-start(bf16[256,4,1024]{2,0,1:T(8,128)(2,1)} %bitcast.43), calls=%async_computation | async-start | bytes 4194304 | tf_op jit(solution)/shard_map/all_to_all | solution.py:49
  39.4 0.0 copy-done.3
  39.4 0.1 dynamic-slice_bitcast_fusion
  39.5 0.2 reduce_window_sum.34
  39.7 0.1 iota_add_fusion
  39.8 0.1 select_reduce_fusion.3
  39.9 0.1 ge.24
  40.0 47.6 %all-to-all-done = bf16[256,4,1024]{2,0,1:T(8,128)(2,1)S(1)} async-done(((bf16[256,4,1024]{2,0,1:T(8,128)(2,1)}), bf16[256,4,1024]{2,0,1:T(8,128)(2,1)S(1)}, u32[]{:S(2)}, u32[]{:S(2)}) %all-to-all-start) | async-done | bytes 2097184 | tf_op jit(solution)/shard_map/all_to_all | solution.py:49
  87.6 2.8 %gather_fusion = bf16[16,128,1024]{2,1,0:T(8,128)(2,1)} fusion(bf16[8,128,1024]{2,1,0:T(8,128)(2,1)S(1)} %bitcast.41, s32[1024]{0:T(1024)S(1)} %pad_clamp_fusion.2), kind=kCustom, calls=%fused_computation.2 | custom fusion | bytes 8388672 | tf_op jit(solution)/shard_map/gather | solution.py:87
  90.4 4.5 %broadcast_select_fusion = bf16[4,4,128,1024]{3,2,1,0:T(8,128)(2,1)} fusion(bf16[4,4,128,1024]{3,2,1,0:T(8,128)(2,1)} %bitcast.42, pred[4,4]{1,0:T(4,128)(4,1)S(1)} %ge.24), kind=kLoop, calls=%fused_computation.12 | loop fusion | flops 2097152 | bytes 8388624 | tf_op jit(solution)/shard_map/jit(_where)/select_n | solution.py:85
  95.0 4.9 %all-to-all-start.1 = ((bf16[4,4,128,1024]{3,2,1,0:T(8,128)(2,1)}), bf16[4,4,128,1024]{3,2,1,0:T(8,128)(2,1)}, u32[]{:S(2)}, u32[]{:S(2)}) async-start(bf16[4,4,128,1024]{3,2,1,0:T(8,128)(2,1)} %broadcast_select_fusion), calls=%async_computation.1 | async-start | bytes 8388608 | tf_op jit(solution)/shard_map/all_to_all | solution.py:91
  99.9 0.6 broadcast.200
  100.5 0.7 reduce.3
  101.2 0.1 eq.87
  101.3 0.7 reduce_window_sum.35
  102.0 0.1 reshape.103
  102.1 0.1 fusion.15
  102.2 0.1 reduce_window_sum.33
  102.2 0.0 copy-done
  102.3 0.2 select_reduce_fusion.1
  102.5 0.7 gather_fusion.2
  103.2 0.1 select_reduce_fusion
  103.3 0.7 gather_fusion.3
  104.1 0.1 broadcast_bitcast_fusion
  104.1 43.9 %all-to-all-done.1 = bf16[4,4,128,1024]{3,2,1,0:T(8,128)(2,1)} async-done(((bf16[4,4,128,1024]{3,2,1,0:T(8,128)(2,1)}), bf16[4,4,128,1024]{3,2,1,0:T(8,128)(2,1)}, u32[]{:S(2)}, u32[]{:S(2)}) %all-to-all-start.1) | async-done | bytes 4194336 | tf_op jit(solution)/shard_map/all_to_all | solution.py:91
  148.1 7.1 %gather_fusion.1 = bf16[32,128,1024]{2,1,0:T(8,128)(2,1)} fusion(bf16[16,128,1024]{2,1,0:T(8,128)(2,1)} %bitcast.10, s32[1024]{0:T(1024)S(1)} %pad_clamp_fusion), kind=kCustom, calls=%fused_computation.3 | custom fusion | bytes 16777344 | tf_op jit(solution)/shard_map/gather | solution.py:99
  155.2 0.0 copy-start.4
  155.2 7.7 %fusion = f32[4096]{0:T(1024)S(1)} fusion(bf16[4096,1024]{1,0:T(8,128)(2,1)} %param.16, bf16[32,128,1024]{2,1,0:T(8,128)(2,1)} %gather_fusion.1, pred[4096]{0:T(1024)(128)(4,1)S(1)} %broadcast_bitcast_fusion), kind=kLoop, calls=%fused_computation.6 | loop fusion | flops 16773120 | bytes 16797696 | tf_op jit(solution)/shard_map/reduce_sum | solution.py:27
  162.9 35.3 %psum.7 = f32[4096]{0:T(1024)S(1)} all-reduce(f32[4096]{0:T(1024)S(1)} %fusion), channel_id=1, replica_groups=mesh['dp'=4,'seq'=4,'tensor'=2] {'seq','tensor'}, use_global_device_ids=true, to_apply=%region_11.13 | all-reduce | flops 4096 | bytes 32768 | tf_op jit(solution)/shard_map/psum | solution.py:104
  198.2 0.0 copy-done.4
  198.2 10.2 %fusion.2 = bf16[4096,1024]{1,0:T(8,128)(2,1)} fusion(f32[1024]{0:T(1024)S(1)} %copy-done.4, f32[4096]{0:T(1024)S(1)} %add_rsqrt_fusion, bf16[4096,1024]{1,0:T(8,128)(2,1)} %param.16, bf16[32,128,1024]{2,1,0:T(8,128)(2,1)} %gather_fusion.1, pred[4096]{0:T(1024)(128)(4,1)S(1)} %broadcast_bitcast_fusion), kind=kLoop, calls=%fused_computation.8 | loop fusion | flops 20971520 | bytes 25190400 | tf_op jit(solution)/shard_map/convert_element_type | solution.py:106
  (20 shorter events, 0.2 us)
Async XLA Ops:
  0.0 102.2 %copy-start = (s32[4,32]{1,0:T(4,128)S(1)}, s32[4,32]{1,0:T(4,128)}, u32[]{:S(2)}) copy-start(s32[4,32]{1,0:T(4,128)} %param.19) | copy-start | bytes 1540
  0.0 18.2 %copy-start.2 = (f32[4,1024]{1,0:T(4,128)S(1)}, f32[4,1024]{1,0:T(4,128)}, u32[]{:S(2)}) copy-start(f32[4,1024]{1,0:T(4,128)} %param.15) | copy-start | bytes 49156
  0.0 18.2 %copy-start.1 = (bf16[256,3200]{1,0:T(8,128)(2,1)S(1)}, bf16[256,3200]{1,0:T(8,128)(2,1)}, u32[]{:S(2)}) copy-start(bf16[256,3200]{1,0:T(8,128)(2,1)} %param.11) | copy-start | bytes 4915204
  0.0 19.1 %copy-start.5 = (f32[3200]{0:T(1024)S(1)}, f32[3200]{0:T(1024)}, u32[]{:S(2)}) copy-start(f32[3200]{0:T(1024)} %param.13) | copy-start | bytes 38404
  0.0 19.2 %copy-start.6 = (f32[3200]{0:T(1024)S(1)}, f32[3200]{0:T(1024)}, u32[]{:S(2)}) copy-start(f32[3200]{0:T(1024)} %param.12) | copy-start | bytes 38404
  31.5 7.9 %copy-start.3 = (s32[32,1]{0,1:T(1,128)S(1)}, s32[32,1]{0,1:T(1,128)}, u32[]{:S(2)}) copy-start(s32[32,1]{0,1:T(1,128)} %param.18) | copy-start | bytes 388
  33.0 54.6 %all-to-all-start = ((bf16[256,4,1024]{2,0,1:T(8,128)(2,1)}), bf16[256,4,1024]{2,0,1:T(8,128)(2,1)S(1)}, u32[]{:S(2)}, u32[]{:S(2)}) async-start(bf16[256,4,1024]{2,0,1:T(8,128)(2,1)} %bitcast.43), calls=%async_computation | async-start | bytes 4194304 | tf_op jit(solution)/shard_map/all_to_all | solution.py:49
  95.0 53.1 %all-to-all-start.1 = ((bf16[4,4,128,1024]{3,2,1,0:T(8,128)(2,1)}), bf16[4,4,128,1024]{3,2,1,0:T(8,128)(2,1)}, u32[]{:S(2)}, u32[]{:S(2)}) async-start(bf16[4,4,128,1024]{3,2,1,0:T(8,128)(2,1)} %broadcast_select_fusion), calls=%async_computation.1 | async-start | bytes 8388608 | tf_op jit(solution)/shard_map/all_to_all | solution.py:91
  155.2 43.0 %copy-start.4 = (f32[1024]{0:T(1024)S(1)}, f32[1024]{0:T(1024)}, u32[]{:S(2)}) copy-start(f32[1024]{0:T(1024)} %param.17) | copy-start | bytes 12292
where the time goes:
time: 209 us; the launch traced here: 208 us
  waiting for transfers between devices  91.6 us (44%)
  blocking collectives  35.3 us (17%)
  local copies, waits for them, and re-layouts  32.1 us (15%)
  other arithmetic  25.8 us (12%)
  matrix products  12.3 us (6%)
  starting transfers between devices  11.3 us (5%)
    all_to_all x1, waiting for transfers between devices, local(): lax.all_to_all(projected.reshape(local_rows, owners, column_block), 'seq'...  47.6 us
    all_to_all x1, waiting for transfers between devices, local(): lax.all_to_all(outgoing, 'dp', split_axis=0, concat_axis=0, tiled=True)  43.9 us
    psum x1, blocking collectives, local(): totals = lax.psum(squares, ('seq', 'tensor'))  35.3 us
    unnamed x17, local copies, waits for them, and re-layouts  18.8 us
    dot_general x1, matrix products, local(): jnp.dot(normed_in, weights_flat, preferred_element_type=jnp.float32)  12.3 us
    convert_element_type x1, other arithmetic, local(): (assembled.astype(jnp.float32) * scale[:, None] * norm_gain).astype(jnp.b...  10.2 us
    reduce_sum x1, other arithmetic, row_squares(): return jnp.sum(values * values, axis=-1)  7.74 us
    gather x1, local copies, waits for them, and re-layouts, local(): picked = incoming[jnp.clip(arrival_index, 0, replicas * capacity - 1)]  7.11 us
  transfers between devices with their start and end apart: 2, of which 2 were waited for; matrix products, arithmetic and copies ran while one was open for 2% of the time, Pallas kernels for 0%

commit v1 on v0

--- a/solution.py
+++ b/solution.py
@@ -101,7 +101,8 @@
         seq_rows, column_block
     )
     squares = row_squares(assembled)
-    totals = lax.psum(squares, ("seq", "tensor"))
+    terms = lax.all_gather(squares, ("seq", "tensor"))
+    totals = jnp.sum(terms, axis=0)
     scale = lax.rsqrt(totals / D + 1e-05)
     return (assembled.astype(jnp.float32) * scale[:, None] * norm_gain).astype(jnp.bfloat16)
 

time: 209 us -> 204 us (0.976)
  blocking collectives: 35.3 us -> 30.5 us
    psum x1 -> x0, blocking collectives: 35.3 us -> none  [local(): totals = lax.psum(squares, ('seq', 'tensor'))]
    all_gather x0 -> x1, blocking collectives: none -> 30.5 us  [local(): terms = lax.all_gather(squares, ('seq', 'tensor'))]
where the time goes in v1:
time: 204 us
  waiting for transfers between devices  91.6 us (45%)
  local copies, waits for them, and re-layouts  32.1 us (16%)
  blocking collectives  30.5 us (15%)
  other arithmetic  25.8 us (13%)
  matrix products  12.3 us (6%)
  starting transfers between devices  11.3 us (6%)
    all_to_all x1, waiting for transfers between devices, local(): lax.all_to_all(projected.reshape(local_rows, owners, column_block), 'seq'...  47.6 us
    all_to_all x1, waiting for transfers between devices, local(): lax.all_to_all(outgoing, 'dp', split_axis=0, concat_axis=0, tiled=True)  43.9 us
    all_gather x1, blocking collectives, local(): terms = lax.all_gather(squares, ('seq', 'tensor'))  30.5 us
    unnamed x17, local copies, waits for them, and re-layouts  18.8 us
    dot_general x1, matrix products, local(): jnp.dot(normed_in, weights_flat, preferred_element_type=jnp.float32)  12.3 us
    convert_element_type x1, other arithmetic, local(): (assembled.astype(jnp.float32) * scale[:, None] * norm_gain).astype(jnp.b...  10.2 us
    reduce_sum x1, other arithmetic, row_squares(): return jnp.sum(values * values, axis=-1)  7.74 us
    gather x1, local copies, waits for them, and re-layouts, local(): picked = incoming[jnp.clip(arrival_index, 0, replicas * capacity - 1)]  7.11 us
  transfers between devices with their start and end apart: 2, of which 2 were waited for; matrix products, arithmetic and copies ran while one was open for 2% of the time, Pallas kernels for 0%

profile of v1, /device:TPU:0, one launch (start us, length us, event | category | flops | bytes accessed | tf_op | source)
XLA Modules:
  0.0 203.8 jit_solution(11748659698741573480)
XLA Ops:
  0.0 0.0 copy-start
  0.0 0.0 copy-start.2
  0.0 0.0 copy-start.1
  0.0 0.0 copy-start.5
  0.0 0.0 copy-start.6
  0.0 18.2 %copy.14 = bf16[400,8,4,1024]{3,1,2,0:T(8,128)(2,1)} copy(bf16[400,8,4,1024]{3,2,1,0:T(4,128)(2,1)} %bitcast.39) | data formatting | bytes 52428800
  18.2 0.0 copy-done.2
  18.2 0.0 copy-done.1
  18.3 0.3 convert_reduce_fusion
  18.6 0.6 fusion.6
  19.2 0.0 copy-done.5
  19.2 0.0 copy-done.6
  19.2 12.3 %fusion.3 = bf16[256,4096]{1,0:T(8,128)(2,1)S(1)} fusion(bf16[3200,4096]{1,0:T(8,128)(2,1)} %bitcast.40, f32[4096]{0:T(1024)S(1)} %bitcast.46, bf16[256,3200]{1,0:T(8,128)(2,1)S(1)} %copy-done.1, f32[3200]{0:T(1024)S(1)} %copy-done.5, f32[3200]{0:T(1024)S(1)} %copy-done.6, f32[256]{0:T(256)S(1)} %add_rsqrt_fusion.1, f32[256]{0:T(256)S(1)} %broadcast_multiply_fusion), kind=kOutput, calls=%fused_computation.11 | convolution fusion | flops 6717898752 | bytes 29993984 | tf_op jit(solution)/shard_map/dot_general | solution.py:45
  31.5 0.0 copy-start.3
  31.5 1.5 copy.18
  33.0 6.4 %all-to-all-start = ((bf16[256,4,1024]{2,0,1:T(8,128)(2,1)}), bf16[256,4,1024]{2,0,1:T(8,128)(2,1)S(1)}, u32[]{:S(2)}, u32[]{:S(2)}) async-start(bf16[256,4,1024]{2,0,1:T(8,128)(2,1)} %bitcast.43), calls=%async_computation | async-start | bytes 4194304 | tf_op jit(solution)/shard_map/all_to_all | solution.py:49
  39.4 0.0 copy-done.3
  39.4 0.1 dynamic-slice_bitcast_fusion
  39.5 0.2 reduce_window_sum.34
  39.7 0.1 iota_add_fusion
  39.8 0.1 select_reduce_fusion.3
  39.9 0.1 ge.24
  40.0 47.6 %all-to-all-done = bf16[256,4,1024]{2,0,1:T(8,128)(2,1)S(1)} async-done(((bf16[256,4,1024]{2,0,1:T(8,128)(2,1)}), bf16[256,4,1024]{2,0,1:T(8,128)(2,1)S(1)}, u32[]{:S(2)}, u32[]{:S(2)}) %all-to-all-start) | async-done | bytes 2097184 | tf_op jit(solution)/shard_map/all_to_all | solution.py:49
  87.6 2.8 %gather_fusion = bf16[16,128,1024]{2,1,0:T(8,128)(2,1)} fusion(bf16[8,128,1024]{2,1,0:T(8,128)(2,1)S(1)} %bitcast.41, s32[1024]{0:T(1024)S(1)} %pad_clamp_fusion.2), kind=kCustom, calls=%fused_computation.2 | custom fusion | bytes 8388672 | tf_op jit(solution)/shard_map/gather | solution.py:87
  90.4 4.5 %broadcast_select_fusion = bf16[4,4,128,1024]{3,2,1,0:T(8,128)(2,1)} fusion(bf16[4,4,128,1024]{3,2,1,0:T(8,128)(2,1)} %bitcast.42, pred[4,4]{1,0:T(4,128)(4,1)S(1)} %ge.24), kind=kLoop, calls=%fused_computation.12 | loop fusion | flops 2097152 | bytes 8388624 | tf_op jit(solution)/shard_map/jit(_where)/select_n | solution.py:85
  95.0 4.9 %all-to-all-start.1 = ((bf16[4,4,128,1024]{3,2,1,0:T(8,128)(2,1)}), bf16[4,4,128,1024]{3,2,1,0:T(8,128)(2,1)}, u32[]{:S(2)}, u32[]{:S(2)}) async-start(bf16[4,4,128,1024]{3,2,1,0:T(8,128)(2,1)} %broadcast_select_fusion), calls=%async_computation.1 | async-start | bytes 8388608 | tf_op jit(solution)/shard_map/all_to_all | solution.py:91
  99.9 0.6 broadcast.207
  100.5 0.7 reduce.3
  101.2 0.1 eq.87
  101.3 0.7 reduce_window_sum.35
  102.0 0.1 reshape.107
  102.1 0.1 fusion.15
  102.2 0.1 reduce_window_sum.33
  102.2 0.0 copy-done
  102.3 0.2 select_reduce_fusion.1
  102.5 0.7 gather_fusion.2
  103.2 0.1 select_reduce_fusion
  103.3 0.7 gather_fusion.3
  104.1 0.1 broadcast_bitcast_fusion
  104.1 43.9 %all-to-all-done.1 = bf16[4,4,128,1024]{3,2,1,0:T(8,128)(2,1)} async-done(((bf16[4,4,128,1024]{3,2,1,0:T(8,128)(2,1)}), bf16[4,4,128,1024]{3,2,1,0:T(8,128)(2,1)}, u32[]{:S(2)}, u32[]{:S(2)}) %all-to-all-start.1) | async-done | bytes 4194336 | tf_op jit(solution)/shard_map/all_to_all | solution.py:91
  148.1 7.1 %gather_fusion.1 = bf16[32,128,1024]{2,1,0:T(8,128)(2,1)} fusion(bf16[16,128,1024]{2,1,0:T(8,128)(2,1)} %bitcast.10, s32[1024]{0:T(1024)S(1)} %pad_clamp_fusion), kind=kCustom, calls=%fused_computation.3 | custom fusion | bytes 16777344 | tf_op jit(solution)/shard_map/gather | solution.py:99
  155.2 0.0 copy-start.4
  155.2 7.7 %fusion = f32[4096]{0:T(1024)S(1)} fusion(bf16[4096,1024]{1,0:T(8,128)(2,1)} %param.16, bf16[32,128,1024]{2,1,0:T(8,128)(2,1)} %gather_fusion.1, pred[4096]{0:T(1024)(128)(4,1)S(1)} %broadcast_bitcast_fusion), kind=kLoop, calls=%fused_computation.6 | loop fusion | flops 16773120 | bytes 16797696 | tf_op jit(solution)/shard_map/reduce_sum | solution.py:27
  162.9 30.5 %all-gather = f32[32768]{0:T(1024)S(1)} all-gather(f32[4096]{0:T(1024)S(1)} %fusion), channel_id=2, replica_groups=mesh['dp'=4,'seq'=4,'tensor'=2] {'seq','tensor'}, dimensions={0}, use_global_device_ids=true | all-gather | bytes 147456 | tf_op jit(solution)/shard_map/all_gather | solution.py:104
  193.6 0.0 copy-done.4
  193.6 10.2 %fusion.2 = bf16[4096,1024]{1,0:T(8,128)(2,1)} fusion(f32[1024]{0:T(1024)S(1)} %copy-done.4, f32[4096]{0:T(1024)S(1)} %add_rsqrt_fusion, bf16[4096,1024]{1,0:T(8,128)(2,1)} %param.16, bf16[32,128,1024]{2,1,0:T(8,128)(2,1)} %gather_fusion.1, pred[4096]{0:T(1024)(128)(4,1)S(1)} %broadcast_bitcast_fusion), kind=kLoop, calls=%fused_computation.8 | loop fusion | flops 20971520 | bytes 25190400 | tf_op jit(solution)/shard_map/convert_element_type | solution.py:107
  (22 shorter events, 0.3 us)
Async XLA Ops:
  0.0 102.2 %copy-start = (s32[4,32]{1,0:T(4,128)S(1)}, s32[4,32]{1,0:T(4,128)}, u32[]{:S(2)}) copy-start(s32[4,32]{1,0:T(4,128)} %param.19) | copy-start | bytes 1540
  0.0 18.2 %copy-start.2 = (f32[4,1024]{1,0:T(4,128)S(1)}, f32[4,1024]{1,0:T(4,128)}, u32[]{:S(2)}) copy-start(f32[4,1024]{1,0:T(4,128)} %param.15) | copy-start | bytes 49156
  0.0 18.2 %copy-start.1 = (bf16[256,3200]{1,0:T(8,128)(2,1)S(1)}, bf16[256,3200]{1,0:T(8,128)(2,1)}, u32[]{:S(2)}) copy-start(bf16[256,3200]{1,0:T(8,128)(2,1)} %param.11) | copy-start | bytes 4915204
  0.0 19.1 %copy-start.5 = (f32[3200]{0:T(1024)S(1)}, f32[3200]{0:T(1024)}, u32[]{:S(2)}) copy-start(f32[3200]{0:T(1024)} %param.13) | copy-start | bytes 38404
  0.0 19.2 %copy-start.6 = (f32[3200]{0:T(1024)S(1)}, f32[3200]{0:T(1024)}, u32[]{:S(2)}) copy-start(f32[3200]{0:T(1024)} %param.12) | copy-start | bytes 38404
  31.5 7.9 %copy-start.3 = (s32[32,1]{0,1:T(1,128)S(1)}, s32[32,1]{0,1:T(1,128)}, u32[]{:S(2)}) copy-start(s32[32,1]{0,1:T(1,128)} %param.18) | copy-start | bytes 388
  33.0 54.6 %all-to-all-start = ((bf16[256,4,1024]{2,0,1:T(8,128)(2,1)}), bf16[256,4,1024]{2,0,1:T(8,128)(2,1)S(1)}, u32[]{:S(2)}, u32[]{:S(2)}) async-start(bf16[256,4,1024]{2,0,1:T(8,128)(2,1)} %bitcast.43), calls=%async_computation | async-start | bytes 4194304 | tf_op jit(solution)/shard_map/all_to_all | solution.py:49
  95.0 53.1 %all-to-all-start.1 = ((bf16[4,4,128,1024]{3,2,1,0:T(8,128)(2,1)}), bf16[4,4,128,1024]{3,2,1,0:T(8,128)(2,1)}, u32[]{:S(2)}, u32[]{:S(2)}) async-start(bf16[4,4,128,1024]{3,2,1,0:T(8,128)(2,1)} %broadcast_select_fusion), calls=%async_computation.1 | async-start | bytes 8388608 | tf_op jit(solution)/shard_map/all_to_all | solution.py:91
  155.2 38.4 %copy-start.4 = (f32[1024]{0:T(1024)S(1)}, f32[1024]{0:T(1024)}, u32[]{:S(2)}) copy-start(f32[1024]{0:T(1024)} %param.17) | copy-start | bytes 12292
